TPU v7x, 32 devices: a whole 2x2x4 slice. The times are simulated.
32 devices in a mesh: heads: 4 (over x, core), ctx: 8 (over z, y).
Axes of the slice: x: 2, y: 2, z: 4, core: 2. Of those that a mesh axis runs over, the one named last changes fastest.
Arguments:
- queries: bfloat16 [1536, 2048], P('ctx', 'heads'), may hold values from -6 to 6
- key_states: bfloat16 [1536, 512], P('ctx', 'heads'), may hold values from -6 to 6
- value_states: bfloat16 [1536, 512], P('ctx', 'heads'), may hold values from -6 to 6
- attention_out: bfloat16 [1536, 2048], P('ctx', 'heads'), may hold values from -2 to 2
- out_grad: bfloat16 [1536, 2048], P('ctx', 'heads'), may hold values from -6 to 6
- log_sum_exp: float32 [16, 1536], P('heads', 'ctx'), may hold values from 0 to 16, as said below
- block_counts: int32 [8], replicated, may hold values from 1 to 3, as said below
- w_query: bfloat16 [4096, 2048], P(None, 'heads'), may hold values from -0.09375 to 0.09375
- w_key: bfloat16 [4096, 512], P(None, 'heads'), may hold values from -0.09375 to 0.09375
- w_value: bfloat16 [4096, 512], P(None, 'heads'), may hold values from -0.09375 to 0.09375
Outputs:
- input_grad: bfloat16 [1536, 4096], P('ctx', 'heads')
- key_grad: float32 [1536, 512], P('ctx', 'heads')
- value_grad: float32 [1536, 512], P('ctx', 'heads')
Inputs may be any that keep to these rules, and one draw needn't show every extreme that they name: `block_counts`: one entry equals 3. `log_sum_exp`: finite offsets of each row's scores.
All inputs are finite; a program needn't handle non-finite values.
Results may differ from a plain program's by a relative error of at most 0.0063.
Values may be sent and summed in bfloat16 or wider, within the bound.
A program may use at most 128 MiB of HBM per device.

v0:
```python
import math
import jax
import jax.numpy as jnp
from jax import lax
from jax.sharding import PartitionSpec as P

BLOCK = 64


def key_span(row_count, capacity):
    shards = row_count // capacity
    per_step = max(1, min(shards, 512 // capacity))
    while shards % per_step:
        per_step = per_step - 1
    return per_step * capacity


def row_info(row_index, lengths, offsets, capacity):
    device = row_index // capacity
    onehot = device[:, None] == jnp.arange(lengths.shape[0], dtype=jnp.int32)[None, :]
    length = jnp.sum(jnp.where(onehot, lengths[None, :], 0), axis=1)
    offset = jnp.sum(jnp.where(onehot, offsets[None, :], 0), axis=1)
    within = row_index - device * capacity
    return (offset + within, within < length)


def tile_grads(
    query_blk,
    grad_blk,
    norm_blk,
    delta_blk,
    query_pos,
    query_live,
    key_blk,
    value_blk,
    key_pos,
    key_live,
    score_scale,
):
    scores = (
        jnp.einsum("qgd,kd->gqk", query_blk, key_blk, preferred_element_type=jnp.float32)
        * score_scale
    )
    visible = query_live[:, None] & key_live[None, :] & (key_pos[None, :] <= query_pos[:, None])
    probability = jnp.where(visible[None], jnp.exp(scores - norm_blk.T[:, :, None]), 0.0)
    prob_grad = jnp.einsum("qgd,kd->gqk", grad_blk, value_blk, preferred_element_type=jnp.float32)
    score_grad = probability * (prob_grad - delta_blk.T[:, :, None])
    return (probability.astype(jnp.bfloat16), score_grad.astype(jnp.bfloat16))


def on_device(
    queries,
    key_states,
    value_states,
    attention_out,
    out_grad,
    log_sum_exp,
    block_counts,
    w_query,
    w_key,
    w_value,
):
    capacity = key_states.shape[0]
    head_dim = key_states.shape[1]
    group = queries.shape[1] // head_dim
    score_scale = 1.0 / math.sqrt(head_dim)
    own_index = lax.axis_index("ctx")
    lengths = block_counts * BLOCK
    offsets = jnp.cumsum(lengths) - lengths
    own_rows = own_index * capacity + jnp.arange(capacity, dtype=jnp.int32)
    own_pos, own_live = row_info(own_rows, lengths, offsets, capacity)
    query_heads = queries.reshape(capacity, group, head_dim)
    grad_heads = out_grad.reshape(capacity, group, head_dim)
    output_heads = attention_out.reshape(capacity, group, head_dim)
    delta_rows = jnp.sum(grad_heads.astype(jnp.float32) * output_heads.astype(jnp.float32), axis=2)
    norm_rows = log_sum_exp.T
    zero_rows = jnp.zeros((capacity, group, head_dim), jnp.float32)
    zero_own = jnp.zeros((capacity, head_dim), jnp.float32)
    key_piece = lax.all_gather(key_states, "ctx", axis=0, tiled=True)
    value_piece = lax.all_gather(value_states, "ctx", axis=0, tiled=True)
    span = key_span(key_piece.shape[0], capacity)

    def step(block_num, query_grad):
        begin_row = block_num * span
        key_blk = lax.dynamic_slice_in_dim(key_piece, begin_row, span, 0)
        value_blk = lax.dynamic_slice_in_dim(value_piece, begin_row, span, 0)
        key_pos, key_live = row_info(
            begin_row + jnp.arange(span, dtype=jnp.int32), lengths, offsets, capacity
        )

        def compute():
            prob_b, grad_b = tile_grads(
                query_heads,
                grad_heads,
                norm_rows,
                delta_rows,
                own_pos,
                own_live,
                key_blk,
                value_blk,
                key_pos,
                key_live,
                score_scale,
            )
            return score_scale * jnp.einsum(
                "gqk,kd->qgd", grad_b, key_blk, preferred_element_type=jnp.float32
            )

        terms = compute()
        return query_grad + terms

    query_grad = lax.fori_loop(0, key_piece.shape[0] // span, step, zero_rows)
    norm_all, delta_all = (
        lax.all_gather(norm_rows, "ctx", axis=0, tiled=True),
        lax.all_gather(delta_rows, "ctx", axis=0, tiled=True),
    )
    query_piece = lax.all_gather(queries, "ctx", axis=0, tiled=True)
    grad_piece = lax.all_gather(out_grad, "ctx", axis=0, tiled=True)
    fold_span = key_span(query_piece.shape[0], capacity)

    def step(block_num, state):
        key_acc, value_acc = state
        begin_row = block_num * fold_span
        query_blk = lax.dynamic_slice_in_dim(query_piece, begin_row, fold_span, 0).reshape(
            fold_span, group, head_dim
        )
        grad_blk = lax.dynamic_slice_in_dim(grad_piece, begin_row, fold_span, 0).reshape(
            fold_span, group, head_dim
        )
        norm_blk = lax.dynamic_slice_in_dim(norm_all, begin_row, fold_span, 0)
        delta_blk = lax.dynamic_slice_in_dim(delta_all, begin_row, fold_span, 0)
        query_pos, query_live = row_info(
            begin_row + jnp.arange(fold_span, dtype=jnp.int32), lengths, offsets, capacity
        )

        def compute():
            prob_b, grad_b = tile_grads(
                query_blk,
                grad_blk,
                norm_blk,
                delta_blk,
                query_pos,
                query_live,
                key_states,
                value_states,
                own_pos,
                own_live,
                score_scale,
            )
            return (
                score_scale
                * jnp.einsum("gqk,qgd->kd", grad_b, query_blk, preferred_element_type=jnp.float32),
                jnp.einsum("gqk,qgd->kd", prob_b, grad_blk, preferred_element_type=jnp.float32),
            )

        terms = compute()
        return (key_acc + terms[0], value_acc + terms[1])

    key_grad, value_grad = lax.fori_loop(
        0, query_piece.shape[0] // fold_span, step, (zero_own, zero_own)
    )
    query_flat = query_grad.reshape(capacity, group * head_dim).astype(jnp.bfloat16)
    partial_input = jnp.einsum("rc,mc->rm", query_flat, w_query, preferred_element_type=jnp.float32)
    partial_input = partial_input + jnp.einsum(
        "rc,mc->rm", key_grad.astype(jnp.bfloat16), w_key, preferred_element_type=jnp.float32
    )
    partial_input = partial_input + jnp.einsum(
        "rc,mc->rm", value_grad.astype(jnp.bfloat16), w_value, preferred_element_type=jnp.float32
    )
    input_part = lax.psum_scatter(partial_input, "heads", scatter_dimension=1, tiled=True)
    return (input_part.astype(jnp.bfloat16), key_grad, value_grad)


def solution(mesh):
    return jax.shard_map(
        on_device,
        mesh=mesh,
        in_specs=(
            P("ctx", "heads"),
            P("ctx", "heads"),
            P("ctx", "heads"),
            P("ctx", "heads"),
            P("ctx", "heads"),
            P("heads", "ctx"),
            P(),
            P(None, "heads"),
            P(None, "heads"),
            P(None, "heads"),
        ),
        out_specs=(P("ctx", "heads"), P("ctx", "heads"), P("ctx", "heads")),
        check_vma=False,
    )
```

profile of v0, /device:TPU:0, one launch (start us, length us, event | category | flops | bytes accessed | tf_op | source)
XLA Modules:
  0.0 253.6 jit_solution(5064324992087366843)
XLA Ops:
  7.3 0.7 all-gather.5.cloned.1.call-update
  8.0 0.7 all-gather.7.cloned.1.call-update
  8.7 1.0 reshape.280
  9.7 1.0 copy_bitcast_fusion
  10.7 0.7 copy_bitcast_fusion.1
  12.7 0.7 select_reduce_fusion.4
  14.0 0.6 fusion.52
  15.1 34.2 %all_gather.18 = bf16[1536,128]{1,0:T(8,128)(2,1)S(1)} all-gather(bf16[192,128]{1,0:T(8,128)(2,1)} %param.15), channel_id=1, replica_groups=mesh['heads'=4,'ctx'=8] {'ctx'}, dimensions={0}, use_global_device_ids=true | all-gather | bytes 442368 | tf_op jit(solution)/shard_map/all_gather | solution.py:79
  49.3 33.4 %all_gather.19 = bf16[1536,128]{1,0:T(8,128)(2,1)} all-gather(bf16[192,128]{1,0:T(8,128)(2,1)S(1)} %copy-done.3), channel_id=1, replica_groups=mesh['heads'=4,'ctx'=8] {'ctx'}, dimensions={0}, use_global_device_ids=true | all-gather | bytes 442368 | tf_op jit(solution)/shard_map/all_gather | solution.py:80
  82.7 18.1 %while.34 = (s32[]{:T(128)}, f32[192,4,128]{2,0,1:T(8,128)S(1)}, bf16[1536,128]{1,0:T(8,128)(2,1)S(1)}, pred[192]{0:T(512)(128)(4,1)}, s32[8]{0:T(128)}, /*index...) while((s32[]{:T(128)}, f32[192,4,128]{2,0,1:T(8,128)S(1)}, ...), condition=%wide.region_7.8_spmd.clone, body=%wide.region_4.7_spmd.clone.sunk | while | flops 228805248 | bytes 4005340 | solution.py:112
  82.7 0.7 select_reduce_fusion.8
  83.5 0.8 compare_and_fusion.4
  84.3 1.4 fusion.93
  85.7 1.5 fusion.94
  87.3 0.7 select_reduce_fusion.8
  88.0 0.8 compare_and_fusion.4
  88.8 1.4 fusion.93
  90.2 1.5 fusion.94
  91.8 0.7 select_reduce_fusion.8
  92.5 0.8 compare_and_fusion.4
  93.4 1.4 fusion.93
  94.7 1.5 fusion.94
  96.3 0.7 select_reduce_fusion.8
  97.1 0.8 compare_and_fusion.4
  97.9 1.4 fusion.93
  99.3 1.5 fusion.94
  100.9 30.6 %all-gather.1 = f32[8,192,4]{1,2,0:T(4,128)S(1)} all-gather(f32[1,192,4]{1,2,0:T(4,128)S(1)} %copy.55), channel_id=1, replica_groups=mesh['heads'=4,'ctx'=8] {'ctx'}, dimensions={0}, use_global_device_ids=true | all-gather | bytes 27648 | tf_op jit(solution)/shard_map/all_gather | solution.py:115
  131.6 0.7 reshape.285
  132.3 30.6 %all-gather = f32[8,192,4]{1,2,0:T(4,128)S(1)} all-gather(f32[1,192,4]{1,2,0:T(4,128)S(1)} %bitcast.173), channel_id=1, replica_groups=mesh['heads'=4,'ctx'=8] {'ctx'}, dimensions={0}, use_global_device_ids=true | all-gather | bytes 27648 | tf_op jit(solution)/shard_map/all_gather | solution.py:114
  162.9 0.7 reshape.283
  163.6 5.4 %fusion.46 = f32[192,4096]{1,0:T(8,128)} fusion(bf16[4096,512]{1,0:T(8,128)(2,1)} %param.21, f32[192,4,128]{2,0,1:T(8,128)S(1)} %get-tuple-element.600), kind=kOutput, calls=%fused_computation.72 | convolution fusion | flops 805404672 | bytes 7733248 | tf_op jit(solution)/shard_map/rc,mc->rm/dot_general | solution.py:163
  168.9 31.9 %while.35 = (s32[]{:T(128)}, f32[192,128]{1,0:T(8,128)S(1)}, f32[192,128]{1,0:T(8,128)}, s32[8]{0:T(128)}, pred[192]{0:T(512)(128)(4,1)}, /*index=5*/s32[192]{0:...) while((s32[]{:T(128)}, f32[192,128]{1,0:T(8,128)S(1)}, ...), condition=%wide.region_11.12_spmd.clone, body=%wide.region_8.11_spmd.clone.sunk | while | flops 304425600 | bytes 8972294 | solution.py:159
  168.9 0.7 select_reduce_fusion.9
  169.7 0.8 compare_and_fusion.5
  170.5 1.2 constant_dynamic-slice_fusion.3
  171.9 1.3 dynamic-slice_bitcast_fusion.3
  173.2 1.2 fusion.104
  174.6 1.0 fusion.106
  175.6 0.6 fusion.105
  176.3 0.7 select_reduce_fusion.9
  177.0 0.8 compare_and_fusion.5
  177.8 1.2 constant_dynamic-slice_fusion.3
  179.2 1.3 dynamic-slice_bitcast_fusion.3
  180.5 1.2 fusion.104
  182.0 1.9 fusion.106
  183.8 0.6 fusion.105
  184.5 0.7 select_reduce_fusion.9
  185.2 0.8 compare_and_fusion.5
  186.0 1.2 constant_dynamic-slice_fusion.3
  187.4 1.3 dynamic-slice_bitcast_fusion.3
  188.7 1.2 fusion.104
  190.2 1.9 fusion.106
  192.0 0.6 fusion.105
  192.7 0.7 select_reduce_fusion.9
  193.4 0.8 compare_and_fusion.5
  194.3 1.2 constant_dynamic-slice_fusion.3
  195.6 1.3 dynamic-slice_bitcast_fusion.3
  196.9 1.2 fusion.104
  198.4 1.9 fusion.106
  200.3 0.6 fusion.105
  200.9 2.6 %convolution_add_fusion.1 = f32[192,4096]{1,0:T(8,128)S(1)} fusion(f32[192,4096]{1,0:T(8,128)} %fusion.46, bf16[4096,128]{1,0:T(8,128)(2,1)S(1)} %copy-done, f32[192,128]{1,0:T(8,128)S(1)} %get-tuple-element.598), kind=kOutput, calls=%fused_computation.70 | convolution fusion | flops 202137600 | bytes 7438336 | tf_op jit(solution)/shard_map/rc,mc->rm/dot_general | solution.py:164
  203.5 2.2 convolution_add_fusion
  205.8 39.4 %reduce-scatter.2.cloned.1.call-done = f32[192,1024]{1,0:T(8,128)} async-done(((f32[192,4096]{1,0:T(8,128)}), f32[192,1024]{1,0:T(8,128)}) %reduce-scatter.2.cloned.1.call-update) | async-done | bytes 786448 | tf_op jit(solution)/shard_map/reduce_scatter | solution.py:170
  245.1 1.9 convert_element_type.61
  (78 shorter events, 4.7 us)
Async XLA Ops:
  7.2 193.7 %copy-start = (bf16[4096,128]{1,0:T(8,128)(2,1)S(1)}, bf16[4096,128]{1,0:T(8,128)(2,1)}, u32[]{:S(2)}) copy-start(bf16[4096,128]{1,0:T(8,128)(2,1)} %param.22) | copy-start | bytes 3145732
  7.2 3.5 %copy-start.5 = (bf16[192,512]{1,0:T(8,128)(2,1)S(1)}, bf16[192,512]{1,0:T(8,128)(2,1)}, u32[]{:S(2)}) copy-start(bf16[192,512]{1,0:T(8,128)(2,1)} %param.14) | copy-start | bytes 589828
  7.2 4.2 %copy-start.9 = (s32[8]{0:T(128)S(1)}, s32[8]{0:T(128)}, u32[]{:S(2)}) copy-start(s32[8]{0:T(128)} %param.20) | copy-start | bytes 100
  7.2 7.4 %copy-start.7 = (bf16[192,512]{1,0:T(8,128)(2,1)S(1)}, bf16[192,512]{1,0:T(8,128)(2,1)}, u32[]{:S(2)}) copy-start(bf16[192,512]{1,0:T(8,128)(2,1)} %param.17) | copy-start | bytes 589828
  7.2 161.7 %all-gather.5.cloned.1.call-start = ((), (), s32[]{:S(2)}) async-start(), calls=%async_computation.1 | async-start | bytes 1769472 | tf_op jit(solution)/shard_map/all_gather | solution.py:117
  7.9 161.0 %all-gather.7.cloned.1.call-start = ((), (), s32[]{:S(2)}) async-start(), calls=%async_computation.2 | async-start | bytes 1769472 | tf_op jit(solution)/shard_map/all_gather | solution.py:118
  8.7 236.4 %reduce-scatter.2.cloned.1.call-start = ((), (), s32[]{:S(2)}) async-start(), calls=%async_computation.3 | async-start | bytes 3932160 | tf_op jit(solution)/shard_map/reduce_scatter | solution.py:170
  10.7 38.6 %copy-start.3 = (bf16[192,128]{1,0:T(8,128)(2,1)S(1)}, bf16[192,128]{1,0:T(8,128)(2,1)}, u32[]{:S(2)}) copy-start(bf16[192,128]{1,0:T(8,128)(2,1)} %param.16) | copy-start | bytes 147460
  11.4 71.3 %copy-start.8 = (f32[4,192]{1,0:T(4,128)S(1)}, f32[4,192]{1,0:T(4,128)}, u32[]{:S(2)}) copy-start(f32[4,192]{1,0:T(4,128)} %param.19) | copy-start | bytes 9220
  174.6 1.0 copy-start.6
  181.9 1.9 copy-start.6
  190.2 1.9 copy-start.6
  198.4 1.9 copy-start.6
  200.9 2.6 %copy-start.1 = (f32[192,128]{1,0:T(8,128)}, f32[192,128]{1,0:T(8,128)S(1)}, u32[]{:S(2)}) copy-start(f32[192,128]{1,0:T(8,128)S(1)} %get-tuple-element.598) | copy-start | bytes 294916
  200.9 2.6 %copy-start.2 = (f32[192,128]{1,0:T(8,128)S(1)}, f32[192,128]{1,0:T(8,128)}, u32[]{:S(2)}) copy-start(f32[192,128]{1,0:T(8,128)} %get-tuple-element.599) | copy-start | bytes 294916
  200.9 2.6 %copy-start.4 = (bf16[4096,128]{1,0:T(8,128)(2,1)S(1)}, bf16[4096,128]{1,0:T(8,128)(2,1)}, u32[]{:S(2)}) copy-start(bf16[4096,128]{1,0:T(8,128)(2,1)} %param.23) | copy-start | bytes 3145732
Sparse Core Ops, SparseCore 0:
  10.2 50.6 all-gather.4
  63.1 43.6 all-gather.6
  205.9 39.1 reduce-scatter.1
where the time goes:
time: 255 us; the launch traced here: 254 us
  blocking collectives  129 us (51%)
  waiting for transfers between devices  40.8 us (16%)
  matrix products  35.5 us (14%)
  other arithmetic  18 us (7%)
  local copies, waits for them, and re-layouts  16 us (6%)
  between operations  13.9 us (5%)
    reduce_scatter x1, waiting for transfers between devices, on_device(): lax.psum_scatter(partial_input, 'heads', scatter_dimension=1, tiled=True)  39.4 us
    all_gather x1, blocking collectives, on_device(): key_piece = lax.all_gather(key_states, 'ctx', axis=0, tiled=True)  34.2 us
    all_gather x1, blocking collectives, on_device(): value_piece = lax.all_gather(value_states, 'ctx', axis=0, tiled=True)  33.4 us
    all_gather x1, blocking collectives, on_device(): lax.all_gather(delta_rows, 'ctx', axis=0, tiled=True)  30.6 us
    all_gather x1, blocking collectives, on_device(): lax.all_gather(norm_rows, 'ctx', axis=0, tiled=True)  30.6 us
    dot_general x8, matrix products, tile_grads(): jnp.einsum('qgd,kd->gqk', query_blk, key_blk, preferred_element_type=jnp....  10.2 us
    dot_general x4, matrix products, compute(): jnp.einsum('gqk,qgd->kd', prob_b, grad_blk, preferred_element_type=jnp.fl...  6.56 us
    and x8, other arithmetic, tile_grads(): query_live[:, None] & key_live[None, :]  6.44 us
  transfers between devices with their start and end apart: 3, of which 1 were waited for; matrix products, arithmetic and copies ran while one was open for 12% of the time, Pallas kernels for 0%

commit v1 on v0

--- a/solution.py
+++ b/solution.py
@@ -76,7 +76,9 @@
     norm_rows = log_sum_exp.T
     zero_rows = jnp.zeros((capacity, group, head_dim), jnp.float32)
     zero_own = jnp.zeros((capacity, head_dim), jnp.float32)
-    key_piece = lax.all_gather(key_states, "ctx", axis=0, tiled=True)
+    key_piece = jnp.concatenate(
+        lax.all_to_all(jnp.stack([key_states] * lax.axis_size("ctx")), "ctx", 0, 0), axis=0
+    )
     value_piece = lax.all_gather(value_states, "ctx", axis=0, tiled=True)
     span = key_span(key_piece.shape[0], capacity)
 

time: 255 us -> 229 us (0.90)
  blocking collectives: 129 us -> 98.3 us
  starting transfers between devices: 0.11 us -> 7.43 us
    all_gather x1 -> x0, blocking collectives: 34.2 us -> none  [on_device(): key_piece = lax.all_gather(key_states, 'ctx', axis=0, tiled=True)]
    all_to_all x0 -> x1, starting transfers between devices: none -> 7.31 us  [on_device(): lax.all_to_all(jnp.stack([key_states] * lax.axis_size('ctx')), 'ctx', 0, 0)]
    all_gather x1, blocking collectives: 30.6 us -> 33.7 us  [on_device(): lax.all_gather(delta_rows, 'ctx', axis=0, tiled=True)]
  transfers between devices with their start and end apart: 3 -> 4, of which waited for: 1 -> 1; matrix products, arithmetic and copies ran while one was open for 12% -> 14% of each run, Pallas kernels for 0% -> 0%
where the time goes in v1:
time: 229 us; the launch traced here: 228 us
  blocking collectives  98.3 us (43%)
  waiting for transfers between devices  38.3 us (17%)
  matrix products  35.4 us (15%)
  other arithmetic  17.7 us (8%)
  local copies, waits for them, and re-layouts  16.3 us (7%)
  between operations  13.9 us (6%)
  starting transfers between devices  7.43 us (3%)
    reduce_scatter x1, waiting for transfers between devices, on_device(): lax.psum_scatter(partial_input, 'heads', scatter_dimension=1, tiled=True)  36.9 us
    all_gather x1, blocking collectives, on_device(): value_piece = lax.all_gather(value_states, 'ctx', axis=0, tiled=True)  33.8 us
    all_gather x1, blocking collectives, on_device(): lax.all_gather(delta_rows, 'ctx', axis=0, tiled=True)  33.7 us
    all_gather x1, blocking collectives, on_device(): lax.all_gather(norm_rows, 'ctx', axis=0, tiled=True)  30.7 us
    dot_general x8, matrix products, tile_grads(): jnp.einsum('qgd,kd->gqk', query_blk, key_blk, preferred_element_type=jnp....  10.2 us
    all_to_all x1, starting transfers between devices, on_device(): lax.all_to_all(jnp.stack([key_states] * lax.axis_size('ctx')), 'ctx', 0, 0)  7.31 us
    dot_general x4, matrix products, compute(): jnp.einsum('gqk,qgd->kd', prob_b, grad_blk, preferred_element_type=jnp.fl...  6.56 us
    and x8, other arithmetic, tile_grads(): query_live[:, None] & key_live[None, :]  6.34 us
  transfers between devices with their start and end apart: 4, of which 1 were waited for; matrix products, arithmetic and copies ran while one was open for 14% of the time, Pallas kernels for 0%

profile of v1, /device:TPU:0, one launch (start us, length us, event | category | flops | bytes accessed | tf_op | source)
XLA Modules:
  0.0 228.0 jit_solution(17212041036027023935)
XLA Ops:
  7.3 0.7 all-gather.5.cloned.1.call-update
  7.9 1.6 stack.2
  9.5 7.3 %all-to-all-start = ((bf16[8,192,128]{2,1,0:T(8,128)(2,1)}), bf16[8,192,128]{2,1,0:T(8,128)(2,1)S(1)}, u32[]{:S(2)}, u32[]{:S(2)}) async-start(bf16[8,192,128]{2,1,0:T(8,128)(2,1)} %stack.2), calls=%async_computation | async-start | bytes 786432 | tf_op jit(solution)/shard_map/all_to_all | solution.py:80
  16.9 0.7 all-gather.7.cloned.1.call-update
  19.0 0.7 select_reduce_fusion.4
  19.7 0.6 fusion.51
  20.7 0.7 copy.52
  21.4 33.7 %all-gather.1 = f32[8,192,4]{1,2,0:T(4,128)S(1)} all-gather(f32[1,192,4]{1,2,0:T(4,128)S(1)} %copy.55), channel_id=1, replica_groups=mesh['heads'=4,'ctx'=8] {'ctx'}, dimensions={0}, use_global_device_ids=true | all-gather | bytes 27648 | tf_op jit(solution)/shard_map/all_gather | solution.py:117
  55.1 0.7 reshape.291
  55.8 30.7 %all-gather = f32[8,192,4]{1,2,0:T(4,128)S(1)} all-gather(f32[1,192,4]{1,2,0:T(4,128)} %bitcast.4), channel_id=1, replica_groups=mesh['heads'=4,'ctx'=8] {'ctx'}, dimensions={0}, use_global_device_ids=true | all-gather | bytes 27648 | tf_op jit(solution)/shard_map/all_gather | solution.py:116
  86.6 0.7 reshape.289
  87.3 33.8 %all_gather.15 = bf16[1536,128]{1,0:T(8,128)(2,1)} all-gather(bf16[192,128]{1,0:T(8,128)(2,1)S(1)} %copy-done.4), channel_id=1, replica_groups=mesh['heads'=4,'ctx'=8] {'ctx'}, dimensions={0}, use_global_device_ids=true | all-gather | bytes 442368 | tf_op jit(solution)/shard_map/all_gather | solution.py:82
  121.7 0.7 copy_bitcast_fusion.1
  122.4 18.1 %while.34 = (s32[]{:T(128)}, f32[192,4,128]{2,0,1:T(8,128)S(1)}, bf16[1536,128]{1,0:T(8,128)(2,1)S(1)}, pred[192]{0:T(512)(128)(4,1)}, s32[8]{0:T(128)}, /*index...) while((s32[]{:T(128)}, f32[192,4,128]{2,0,1:T(8,128)S(1)}, ...), condition=%wide.region_7.8_spmd.clone, body=%wide.region_4.7_spmd.clone.sunk | while | flops 228805248 | bytes 4016632 | solution.py:114
  122.4 0.7 select_reduce_fusion.8
  123.2 0.8 compare_and_fusion.4
  124.0 1.4 fusion.93
  125.4 1.5 fusion.94
  127.0 0.7 select_reduce_fusion.8
  127.7 0.8 compare_and_fusion.4
  128.5 1.4 fusion.93
  129.9 1.5 fusion.94
  131.5 0.7 select_reduce_fusion.8
  132.3 0.8 compare_and_fusion.4
  133.1 1.4 fusion.93
  134.4 1.5 fusion.94
  136.0 0.7 select_reduce_fusion.8
  136.8 0.8 compare_and_fusion.4
  137.6 1.4 fusion.93
  139.0 1.5 fusion.94
  140.5 5.4 %fusion.46 = f32[192,4096]{1,0:T(8,128)} fusion(bf16[4096,512]{1,0:T(8,128)(2,1)} %param.21, f32[192,4,128]{2,0,1:T(8,128)S(1)} %get-tuple-element.600), kind=kOutput, calls=%fused_computation.72 | convolution fusion | flops 805404672 | bytes 7733248 | tf_op jit(solution)/shard_map/rc,mc->rm/dot_general | solution.py:165
  145.9 31.9 %while.35 = (s32[]{:T(128)}, f32[192,128]{1,0:T(8,128)S(1)}, f32[192,128]{1,0:T(8,128)}, s32[8]{0:T(128)}, pred[192]{0:T(512)(128)(4,1)}, /*index=5*/s32[192]{0:...) while((s32[]{:T(128)}, f32[192,128]{1,0:T(8,128)S(1)}, ...), condition=%wide.region_11.12_spmd.clone, body=%wide.region_8.11_spmd.clone.sunk | while | flops 304425600 | bytes 8972294 | solution.py:161
  145.9 0.7 select_reduce_fusion.9
  146.7 0.8 compare_and_fusion.5
  147.5 1.2 constant_dynamic-slice_fusion.3
  148.9 1.3 dynamic-slice_bitcast_fusion.3
  150.2 1.2 fusion.104
  151.6 1.0 fusion.106
  152.6 0.6 fusion.105
  153.2 0.7 select_reduce_fusion.9
  154.0 0.8 compare_and_fusion.5
  154.8 1.2 constant_dynamic-slice_fusion.3
  156.2 1.3 dynamic-slice_bitcast_fusion.3
  157.5 1.2 fusion.104
  158.9 1.9 fusion.106
  160.8 0.6 fusion.105
  161.4 0.7 select_reduce_fusion.9
  162.2 0.8 compare_and_fusion.5
  163.0 1.2 constant_dynamic-slice_fusion.3
  164.4 1.3 dynamic-slice_bitcast_fusion.3
  165.7 1.2 fusion.104
  167.1 1.9 fusion.106
  169.0 0.6 fusion.105
  169.6 0.7 select_reduce_fusion.9
  170.4 0.8 compare_and_fusion.5
  171.2 1.2 constant_dynamic-slice_fusion.3
  172.6 1.3 dynamic-slice_bitcast_fusion.3
  173.9 1.2 fusion.104
  175.3 1.9 fusion.106
  177.2 0.6 fusion.105
  177.8 2.6 %convolution_add_fusion.1 = f32[192,4096]{1,0:T(8,128)S(1)} fusion(f32[192,4096]{1,0:T(8,128)} %fusion.46, bf16[4096,128]{1,0:T(8,128)(2,1)S(1)} %copy-done, f32[192,128]{1,0:T(8,128)S(1)} %get-tuple-element.598), kind=kOutput, calls=%fused_computation.70 | convolution fusion | flops 202137600 | bytes 7438336 | tf_op jit(solution)/shard_map/rc,mc->rm/dot_general | solution.py:166
  180.4 2.2 convolution_add_fusion
  182.7 36.9 %reduce-scatter.2.cloned.1.call-done = f32[192,1024]{1,0:T(8,128)} async-done(((f32[192,4096]{1,0:T(8,128)}), f32[192,1024]{1,0:T(8,128)}) %reduce-scatter.2.cloned.1.call-update) | async-done | bytes 786448 | tf_op jit(solution)/shard_map/reduce_scatter | solution.py:172
  219.5 1.9 convert_element_type.61
  (88 shorter events, 4.7 us)
Async XLA Ops:
  7.2 170.6 %copy-start = (bf16[4096,128]{1,0:T(8,128)(2,1)S(1)}, bf16[4096,128]{1,0:T(8,128)(2,1)}, u32[]{:S(2)}) copy-start(bf16[4096,128]{1,0:T(8,128)(2,1)} %param.22) | copy-start | bytes 3145732
  7.2 10.5 %copy-start.3 = (bf16[192,512]{1,0:T(8,128)(2,1)S(1)}, bf16[192,512]{1,0:T(8,128)(2,1)}, u32[]{:S(2)}) copy-start(bf16[192,512]{1,0:T(8,128)(2,1)} %param.18) | copy-start | bytes 589828
  7.2 10.6 %copy-start.10 = (s32[8]{0:T(128)S(1)}, s32[8]{0:T(128)}, u32[]{:S(2)}) copy-start(s32[8]{0:T(128)} %param.20) | copy-start | bytes 100
  7.2 13.1 %copy-start.8 = (bf16[192,512]{1,0:T(8,128)(2,1)S(1)}, bf16[192,512]{1,0:T(8,128)(2,1)}, u32[]{:S(2)}) copy-start(bf16[192,512]{1,0:T(8,128)(2,1)} %param.17) | copy-start | bytes 589828
  7.2 138.7 %all-gather.5.cloned.1.call-start = ((), (), s32[]{:S(2)}) async-start(), calls=%async_computation.2 | async-start | bytes 1769472 | tf_op jit(solution)/shard_map/all_gather | solution.py:119
  9.5 112.9 %all-to-all-start = ((bf16[8,192,128]{2,1,0:T(8,128)(2,1)}), bf16[8,192,128]{2,1,0:T(8,128)(2,1)S(1)}, u32[]{:S(2)}, u32[]{:S(2)}) async-start(bf16[8,192,128]{2,1,0:T(8,128)(2,1)} %stack.2), calls=%async_computation | async-start | bytes 786432 | tf_op jit(solution)/shard_map/all_to_all | solution.py:80
  16.9 70.4 %copy-start.4 = (bf16[192,128]{1,0:T(8,128)(2,1)S(1)}, bf16[192,128]{1,0:T(8,128)(2,1)}, u32[]{:S(2)}) copy-start(bf16[192,128]{1,0:T(8,128)(2,1)} %param.16) | copy-start | bytes 147460
  16.9 129.0 %all-gather.7.cloned.1.call-start = ((), (), s32[]{:S(2)}) async-start(), calls=%async_computation.3 | async-start | bytes 1769472 | tf_op jit(solution)/shard_map/all_gather | solution.py:120
  17.6 201.9 %reduce-scatter.2.cloned.1.call-start = ((), (), s32[]{:S(2)}) async-start(), calls=%async_computation.4 | async-start | bytes 3932160 | tf_op jit(solution)/shard_map/reduce_scatter | solution.py:172
  20.3 101.4 %copy-start.6 = (bf16[192,512]{1,0:T(8,128)(2,1)S(1)}, bf16[192,512]{1,0:T(8,128)(2,1)}, u32[]{:S(2)}) copy-start(bf16[192,512]{1,0:T(8,128)(2,1)} %param.14) | copy-start | bytes 589828
  122.4 3.0 %copy-start.9 = (f32[192,4]{0,1:T(4,128)S(1)}, f32[192,4]{0,1:T(4,128)}, u32[]{:S(2)}) copy-start(f32[192,4]{0,1:T(4,128)} %get-tuple-element.1032) | copy-start | bytes 9220 | tf_op jit(solution)/shard_map/while
  126.9 3.0 %copy-start.9 = (f32[192,4]{0,1:T(4,128)S(1)}, f32[192,4]{0,1:T(4,128)}, u32[]{:S(2)}) copy-start(f32[192,4]{0,1:T(4,128)} %get-tuple-element.1032) | copy-start | bytes 9220 | tf_op jit(solution)/shard_map/while
  131.5 3.0 %copy-start.9 = (f32[192,4]{0,1:T(4,128)S(1)}, f32[192,4]{0,1:T(4,128)}, u32[]{:S(2)}) copy-start(f32[192,4]{0,1:T(4,128)} %get-tuple-element.1032) | copy-start | bytes 9220 | tf_op jit(solution)/shard_map/while
  136.0 3.0 %copy-start.9 = (f32[192,4]{0,1:T(4,128)S(1)}, f32[192,4]{0,1:T(4,128)}, u32[]{:S(2)}) copy-start(f32[192,4]{0,1:T(4,128)} %get-tuple-element.1032) | copy-start | bytes 9220 | tf_op jit(solution)/shard_map/while
  151.6 1.0 copy-start.7
  158.9 1.9 copy-start.7
  167.1 1.9 copy-start.7
  175.3 1.9 copy-start.7
  177.8 2.6 %copy-start.1 = (f32[192,128]{1,0:T(8,128)}, f32[192,128]{1,0:T(8,128)S(1)}, u32[]{:S(2)}) copy-start(f32[192,128]{1,0:T(8,128)S(1)} %get-tuple-element.598) | copy-start | bytes 294916
  177.8 2.6 %copy-start.2 = (f32[192,128]{1,0:T(8,128)S(1)}, f32[192,128]{1,0:T(8,128)}, u32[]{:S(2)}) copy-start(f32[192,128]{1,0:T(8,128)} %get-tuple-element.599) | copy-start | bytes 294916
  177.8 2.6 %copy-start.5 = (bf16[4096,128]{1,0:T(8,128)(2,1)S(1)}, bf16[4096,128]{1,0:T(8,128)(2,1)}, u32[]{:S(2)}) copy-start(bf16[4096,128]{1,0:T(8,128)(2,1)} %param.23) | copy-start | bytes 3145732
Sparse Core Ops, SparseCore 0:
  10.2 50.0 all-gather.4
  62.5 45.3 all-gather.6
  182.8 36.6 reduce-scatter.1
